TPU v7x, 32 devices: a whole 2x2x4 slice. The times are simulated.
32 devices in a mesh: grp: 2 (over x), freq: 16 (over z, y, core).
Axes of the slice: x: 2, y: 2, z: 4, core: 2. Of those that a mesh axis runs over, the one named last changes fastest.
Arguments:
- kernel: bfloat16 [2, 256, 1024, 1024], P(None, ('grp', 'freq')), parts along dimension 1, may hold values from -0.125 to 0.125
- recorded: float32 [2, 256, 1024, 128], P(None, ('grp', 'freq')), parts along dimension 1, may hold values from -8 to 8
- onset_time: int32 [2048, 128], P(('grp', 'freq')), parts along dimension 0, may hold values from 32 to 256, as said below
Outputs:
- focusing: float32 [256, 2048, 128], P(None, ('grp', 'freq')), parts along dimension 1
There are 2 independent parts, one for each index of `grp`. A program takes and returns all parts, laid end to end along the dimension named above; each array names one. Nothing has to cross between parts.
Inputs may be any that keep to these rules, and one draw needn't show every extreme that they name: `onset_time`: onset sample of the window for each receiver and focal point.
All inputs are finite; a program needn't handle non-finite values.
Results may differ from a plain program's by a relative error of at most 0.012.
Values may be sent and summed in bfloat16 or wider, within the bound.
A program may use at most 192 MiB of HBM per device.

v0:
```python
import math
import jax
import jax.numpy as jnp
from jax import lax
from jax.sharding import PartitionSpec as P

NF = 128
ITERS = 2


def dft_tables():
    samples = jnp.arange(2 * NF, dtype=jnp.int32)
    bins = jnp.arange(NF, dtype=jnp.int32)
    phase = (bins[:, None] * samples[None, :] % (2 * NF)).astype(jnp.float32) * (math.pi / NF)
    factor = 1.0 / math.sqrt(NF)
    return (jnp.cos(phase) * factor, jnp.sin(phase) * factor)


def square_sum(values):
    return jnp.sum(values * values)


def joint_total(first, second, third):
    return lax.psum((first, second, third), "freq")


def body(kernel, recorded, onset_time):
    highest = lax.Precision.HIGHEST
    cosine_table, sin_tab = dft_tables()
    rec_local = onset_time.shape[0]
    focal_count = onset_time.shape[1]
    samples = lax.broadcasted_iota(jnp.int32, (2 * NF, rec_local, focal_count), 0)
    keep_mask = (samples < onset_time[None]).astype(jnp.float32)
    kernel_real = kernel[0]
    kernel_imaginary = kernel[1]

    def invert(block_in):
        columns = block_in.shape[3]
        widened = block_in.astype(jnp.float32)
        timed = jnp.dot(cosine_table.T, widened[0].reshape(NF, -1), precision=highest) - jnp.dot(
            sin_tab.T, widened[1].reshape(NF, -1), precision=highest
        )
        return timed.reshape(2 * NF, block_in.shape[2], columns)

    def apply_adjoint(resid):
        rounded = resid.astype(jnp.bfloat16)
        update_real = rounded[0]
        update_imaginary = rounded[1]
        z_real = jnp.einsum(
            "hvi,hvg->hig", kernel_real, update_real, preferred_element_type=jnp.float32
        ) + jnp.einsum(
            "hvi,hvg->hig", kernel_imaginary, update_imaginary, preferred_element_type=jnp.float32
        )
        z_imag = jnp.einsum(
            "hvi,hvg->hig", kernel_real, update_imaginary, preferred_element_type=jnp.float32
        ) - jnp.einsum(
            "hvi,hvg->hig", kernel_imaginary, update_real, preferred_element_type=jnp.float32
        )
        image = jnp.stack([z_real, z_imag]).astype(jnp.bfloat16)
        timed = invert(lax.all_to_all(image, "freq", split_axis=2, concat_axis=1, tiled=True))
        return timed * keep_mask

    model_raw = apply_adjoint(recorded)
    totals = joint_total(square_sum(recorded), square_sum(model_raw), jnp.float32(0.0))
    beta_now = jnp.sqrt(totals[0])
    data_vec = recorded / beta_now
    alpha_now = jnp.sqrt(totals[1]) / beta_now
    model_vec = model_raw / (alpha_now * beta_now)
    search = model_vec
    estimate = jnp.zeros_like(model_vec)
    phibar_now = beta_now
    rhobar_now = alpha_now
    for iteration in range(ITERS):
        flat_part = (model_vec * keep_mask).reshape(2 * NF, -1)
        spec_real = jnp.dot(cosine_table, flat_part, precision=highest)
        spec_imag = -jnp.dot(sin_tab, flat_part, precision=highest)
        spectrum = (
            jnp.stack([spec_real, spec_imag])
            .reshape(2, NF, rec_local, focal_count)
            .astype(jnp.bfloat16)
        )
        multiply_block_in = lax.all_to_all(
            spectrum, "freq", split_axis=1, concat_axis=2, tiled=True
        )
        solution_real = multiply_block_in[0]
        solution_imaginary = multiply_block_in[1]
        y_real = jnp.einsum(
            "ptx,pxi->pti", kernel_real, solution_real, preferred_element_type=jnp.float32
        ) - jnp.einsum(
            "ptx,pxi->pti", kernel_imaginary, solution_imaginary, preferred_element_type=jnp.float32
        )
        y_imag = jnp.einsum(
            "ptx,pxi->pti", kernel_real, solution_imaginary, preferred_element_type=jnp.float32
        ) + jnp.einsum(
            "ptx,pxi->pti", kernel_imaginary, solution_real, preferred_element_type=jnp.float32
        )
        data_raw = jnp.stack([y_real, y_imag]) - alpha_now * data_vec
        image_raw = apply_adjoint(data_raw)
        totals = joint_total(
            square_sum(data_raw), square_sum(image_raw), jnp.sum(image_raw * model_vec)
        )
        beta_now = jnp.sqrt(totals[0])
        data_vec = data_raw / beta_now
        alpha_now = jnp.sqrt(
            totals[1] / (beta_now * beta_now) - 2.0 * totals[2] + beta_now * beta_now
        )
        model_vec = (image_raw / beta_now - beta_now * model_vec) / alpha_now
        rho_now = jnp.sqrt(rhobar_now * rhobar_now + beta_now * beta_now)
        cosine = rhobar_now / rho_now
        sine_part = beta_now / rho_now
        theta_now = sine_part * alpha_now
        rhobar_now = -cosine * alpha_now
        phi_now = cosine * phibar_now
        phibar_now = sine_part * phibar_now
        estimate = estimate + phi_now / rho_now * search
        search = model_vec - theta_now / rho_now * search
    return estimate


def solution(mesh):
    placed = (
        P(None, ("grp", "freq"), None, None),
        P(None, ("grp", "freq"), None, None),
        P(("grp", "freq"), None),
    )
    return jax.shard_map(
        body, mesh=mesh, in_specs=placed, out_specs=P(None, ("grp", "freq"), None), check_vma=False
    )
```

profile of v0, /device:TPU:0, one launch (start us, length us, event | category | flops | bytes accessed | tf_op | source)
XLA Modules:
  0.0 832.4 jit_solution(1631037788863570241)
XLA Ops:
  8.5 10.8 %fusion.14 = f32[8,1024,128]{2,1,0:T(8,128)} fusion(bf16[2,8,1024,1024]{3,2,1,0:T(8,128)(2,1)} %param.3, bf16[2,8,1024,128]{3,2,1,0:T(8,128)(2,1)S(1)} %get-tuple-element.15), kind=kOutput, calls=%fused_computation.14 | convolution fusion | flops 2147483648 | bytes 23068672 | tf_op jit(solution)/shard_map/hvi,hvg->hig/dot_general | solution.py:51
  19.4 10.7 %fusion.12 = f32[8,1024,128]{2,1,0:T(8,128)} fusion(bf16[2,8,1024,1024]{3,2,1,0:T(8,128)(2,1)} %param.3, bf16[2,8,1024,128]{3,2,1,0:T(8,128)(2,1)S(1)} %get-tuple-element.15), kind=kOutput, calls=%fused_computation.12 | convolution fusion | flops 2147483648 | bytes 23068672 | tf_op jit(solution)/shard_map/hvi,hvg->hig/dot_general | solution.py:56
  39.7 10.4 %fusion.68 = bf16[1,8,1024,128]{3,2,1,0:T(8,128)(2,1)S(1)} fusion(f32[8,1024,128]{2,1,0:T(8,128)} %fusion.12, bf16[2,8,1024,128]{3,2,1,0:T(8,128)(2,1)S(1)} %get-tuple-element.15, bf16[2,8,1024,1024]{3,2,1,0:T(8,128)(2,1)} %param.3), kind=kOutput, calls=%fused_computation.98 | convolution fusion | flops 2149580800 | bytes 25165824 | tf_op jit(solution)/shard_map/hvi,hvg->hig/dot_general | solution.py:54
  53.2 99.3 %all_to_all.60 = bf16[2,8,1024,128]{3,1,0,2:T(8,128)(2,1)S(1)} all-to-all(bf16[2,8,1024,128]{3,1,0,2:T(8,128)(2,1)S(1)} %copy.81), channel_id=1, replica_groups=mesh['grp'=2,'freq'=16] {'freq'}, dimensions={2} | all-to-all | bytes 8388608 | tf_op jit(solution)/shard_map/all_to_all | solution.py:60
  159.0 12.1 %multiply_reduce_fusion.4 = (f32[]{:T(128)}, f32[256,8192]{1,0:T(8,128)}) fusion(s32[8192]{0:T(1024)S(1)} %bitcast.250, f32[256,8192]{1,0:T(8,128)S(1)} %fusion.78, bf16[16,8,64,128]{3,2,1,0:T(8,128)(2,1)S(1)} %get-tuple-element.22), kind=kOutput, calls=%fused_computation.58 | convolution fusion | flops 3232202752 | bytes 18907140 | tf_op jit(solution)/shard_map/dot_general | solution.py:40
  171.1 34.1 %all-reduce.1 = (f32[]{:T(128)}, f32[]{:T(128)}) all-reduce(f32[]{:T(128)} %get-tuple-element.24, f32[]{:T(128)} %get-tuple-element.14), channel_id=1, replica_groups=mesh['grp'=2,'freq'=16] {'freq'}, use_global_device_ids=true, to_apply=%region_1.2 | all-reduce | flops 2 | bytes 16 | tf_op jit(solution)/shard_map/psum | solution.py:24
  206.5 10.7 %fusion.89 = bf16[16,8,64,128]{3,1,2,0:T(8,128)(2,1)S(1)} fusion(s32[8192]{0:T(1024)S(1)} %bitcast.251, f32[256,8192]{1,0:T(8,128)} %get-tuple-element.25, f32[]{:T(128)S(6)} %mul.210), kind=kOutput, calls=%fused_computation.123 | convolution fusion | flops 3231154176 | bytes 10518532 | tf_op jit(solution)/shard_map/dot_general | solution.py:75
  242.5 68.8 %all-to-all-done.1 = bf16[2,128,64,128]{3,2,0,1:T(8,128)(2,1)} async-done(((bf16[2,128,64,128]{3,2,0,1:T(8,128)(2,1)}), bf16[2,128,64,128]{3,2,0,1:T(8,128)(2,1)}, u32[]{:S(2)}, u32[]{:S(2)}) %all-to-all-start.1) | async-done | bytes 4194336 | tf_op jit(solution)/shard_map/all_to_all | solution.py:82
  316.9 14.0 %fusion.10 = f32[8,128,1024]{2,1,0:T(8,128)} fusion(bf16[8,1024,128]{2,1,0:T(8,128)(2,1)} %bitcast.241, bf16[2,8,1024,1024]{3,2,1,0:T(8,128)(2,1)} %param.3), kind=kOutput, calls=%fused_computation.10 | convolution fusion | flops 2147483648 | bytes 23068672 | tf_op jit(solution)/shard_map/ptx,pxi->pti/dot_general | solution.py:89
  332.5 14.0 %fusion.8 = f32[8,128,1024]{2,1,0:T(8,128)} fusion(bf16[8,1024,128]{2,1,0:T(8,128)(2,1)} %bitcast.246, bf16[2,8,1024,1024]{3,2,1,0:T(8,128)(2,1)} %param.3), kind=kOutput, calls=%fused_computation.8 | convolution fusion | flops 2147483648 | bytes 23068672 | tf_op jit(solution)/shard_map/ptx,pxi->pti/dot_general | solution.py:94
  346.5 10.8 %subtract_bitcast_fusion.1 = f32[1,8,1024,128]{2,3,1,0:T(8,128)S(1)} fusion(f32[8,128,1024]{2,1,0:T(8,128)} %fusion.10, bf16[8,1024,128]{2,1,0:T(8,128)(2,1)} %bitcast.247, bf16[2,8,1024,1024]{3,2,1,0:T(8,128)(2,1)} %param.3), kind=kOutput, calls=%fused_computation.74 | convolution fusion | flops 2148532224 | bytes 27262976 | tf_op jit(solution)/shard_map/ptx,pxi->pti/dot_general | solution.py:87
  357.3 11.2 %add_bitcast_fusion.1 = f32[1,8,1024,128]{2,3,1,0:T(8,128)} fusion(f32[8,128,1024]{2,1,0:T(8,128)} %fusion.8, bf16[8,1024,128]{2,1,0:T(8,128)(2,1)S(1)} %bitcast.242, bf16[2,8,1024,1024]{3,2,1,0:T(8,128)(2,1)} %param.3), kind=kOutput, calls=%fused_computation.73 | convolution fusion | flops 2148532224 | bytes 27262976 | tf_op jit(solution)/shard_map/ptx,pxi->pti/dot_general | solution.py:92
  378.8 10.1 %fusion.6 = f32[8,128,1024]{2,1,0:T(8,128)} fusion(bf16[2,8,1024,1024]{3,2,1,0:T(8,128)(2,1)} %param.3, bf16[2,8,1024,128]{2,3,1,0:T(8,128)(2,1)S(1)} %convert_element_type.32), kind=kOutput, calls=%fused_computation.6 | convolution fusion | flops 2147483648 | bytes 23068672 | tf_op jit(solution)/shard_map/hvi,hvg->hig/dot_general | solution.py:51
  388.9 10.1 %fusion.4 = f32[8,128,1024]{2,1,0:T(8,128)} fusion(bf16[2,8,1024,1024]{3,2,1,0:T(8,128)(2,1)} %param.3, bf16[2,8,1024,128]{2,3,1,0:T(8,128)(2,1)S(1)} %convert_element_type.32), kind=kOutput, calls=%fused_computation.4 | convolution fusion | flops 2147483648 | bytes 23068672 | tf_op jit(solution)/shard_map/hvi,hvg->hig/dot_general | solution.py:56
  408.5 10.8 %fusion.70 = bf16[1,8,1024,128]{2,3,1,0:T(8,128)(2,1)} fusion(f32[8,128,1024]{2,1,0:T(8,128)} %fusion.4, bf16[2,8,1024,1024]{3,2,1,0:T(8,128)(2,1)} %param.3, bf16[2,8,1024,128]{2,3,1,0:T(8,128)(2,1)S(1)} %convert_element_type.32), kind=kOutput, calls=%fused_computation.100 | convolution fusion | flops 2149580800 | bytes 25165824 | tf_op jit(solution)/shard_map/hvi,hvg->hig/dot_general | solution.py:54
  430.2 112.1 %all_to_all.61 = bf16[2,8,1024,128]{3,1,0,2:T(8,128)(2,1)S(1)} all-to-all(bf16[2,8,1024,128]{3,1,0,2:T(8,128)(2,1)} %copy.101), channel_id=1, replica_groups=mesh['grp'=2,'freq'=16] {'freq'}, dimensions={2} | all-to-all | bytes 8388608 | tf_op jit(solution)/shard_map/all_to_all | solution.py:60
  549.1 11.3 %multiply_reduce_fusion = (f32[]{:T(128)}, f32[]{:T(128)}, f32[256,8192]{1,0:T(8,128)}) fusion(s32[8192]{0:T(1024)S(1)} %bitcast.253, f32[]{:T(128)S(6)} %mul.210, f32[256,8192]{1,0:T(8,128)S(1)} %bitcast.229, f32[256,8192]{1,0:T(8,128)S(1)} %fusion.73, bf16[16,8,64,128]{3,2,1,0:T(8,128)(2,1)S(1)} %bitcast.245), kind=kOutput, calls=%fused_computation.53 | convolution fusion | flops 3240591360 | bytes 27295756 | tf_op jit(solution)/shard_map/dot_general | solution.py:40
  560.4 34.2 %all-reduce = (f32[]{:T(128)}, f32[]{:T(128)}, f32[]{:T(128)}) all-reduce(f32[]{:T(128)} %get-tuple-element.12, f32[]{:T(128)} %get-tuple-element.6, f32[]{:T(128)} %get-tuple-element.5), channel_id=1, replica_groups=mesh['grp'=2,'freq'=16] {'freq'}, use_global_device_ids=true, to_apply=%region_5.6 | all-reduce | flops 3 | bytes 24 | tf_op jit(solution)/shard_map/psum | solution.py:24
  632.4 68.8 %all-to-all-done.3 = bf16[2,128,64,128]{3,2,0,1:T(8,128)(2,1)} async-done(((bf16[2,128,64,128]{3,2,0,1:T(8,128)(2,1)}), bf16[2,128,64,128]{3,2,0,1:T(8,128)(2,1)}, u32[]{:S(2)}, u32[]{:S(2)}) %all-to-all-start.3) | async-done | bytes 4194336 | tf_op jit(solution)/shard_map/all_to_all | solution.py:82
  706.8 14.0 %fusion.2 = f32[8,128,1024]{2,1,0:T(8,128)} fusion(bf16[8,1024,128]{2,1,0:T(8,128)(2,1)} %bitcast.243, bf16[2,8,1024,1024]{3,2,1,0:T(8,128)(2,1)} %param.3), kind=kOutput, calls=%fused_computation.2 | convolution fusion | flops 2147483648 | bytes 23068672 | tf_op jit(solution)/shard_map/ptx,pxi->pti/dot_general | solution.py:89
  722.4 14.3 %fusion = f32[8,128,1024]{2,1,0:T(8,128)} fusion(bf16[8,1024,128]{2,1,0:T(8,128)(2,1)} %bitcast.248, bf16[2,8,1024,1024]{3,2,1,0:T(8,128)(2,1)} %param.3), kind=kOutput, calls=%fused_computation | convolution fusion | flops 2147483648 | bytes 23068672 | tf_op jit(solution)/shard_map/ptx,pxi->pti/dot_general | solution.py:94
  736.8 10.7 %subtract_bitcast_fusion = f32[1,8,1024,128]{2,3,1,0:T(8,128)S(1)} fusion(f32[8,128,1024]{2,1,0:T(8,128)} %fusion.2, bf16[8,1024,128]{2,1,0:T(8,128)(2,1)} %bitcast.249, bf16[2,8,1024,1024]{3,2,1,0:T(8,128)(2,1)} %param.3), kind=kOutput, calls=%fused_computation.70 | convolution fusion | flops 2148532224 | bytes 27262976 | tf_op jit(solution)/shard_map/ptx,pxi->pti/dot_general | solution.py:87
  747.4 11.2 %add_bitcast_fusion = f32[1,8,1024,128]{2,3,1,0:T(8,128)} fusion(f32[8,128,1024]{2,1,0:T(8,128)} %fusion, bf16[8,1024,128]{2,1,0:T(8,128)(2,1)S(1)} %bitcast.244, bf16[2,8,1024,1024]{3,2,1,0:T(8,128)(2,1)} %param.3), kind=kOutput, calls=%fused_computation.69 | convolution fusion | flops 2148532224 | bytes 27262976 | tf_op jit(solution)/shard_map/ptx,pxi->pti/dot_general | solution.py:92
  773.2 48.3 %psum.47 = f32[]{:T(128)} all-reduce(f32[]{:T(128)} %fusion.40), channel_id=1, replica_groups=mesh['grp'=2,'freq'=16] {'freq'}, use_global_device_ids=true, to_apply=%region_11.12 | all-reduce | flops 1 | bytes 8 | tf_op jit(solution)/shard_map/psum | solution.py:24
  (60 shorter events, 164.4 us)
Async XLA Ops:
  154.5 4.4 copy-start.4
  206.5 10.7 %copy-start = (f32[256,8192]{1,0:T(8,128)S(1)}, f32[256,8192]{1,0:T(8,128)}, u32[]{:S(2)}) copy-start(f32[256,8192]{1,0:T(8,128)} %get-tuple-element.25) | copy-start | bytes 25165828
  229.2 82.0 %all-to-all-start.1 = ((bf16[2,128,64,128]{3,2,0,1:T(8,128)(2,1)}), bf16[2,128,64,128]{3,2,0,1:T(8,128)(2,1)}, u32[]{:S(2)}, u32[]{:S(2)}) async-start(bf16[2,128,64,128]{3,2,0,1:T(8,128)(2,1)} %pad_maximum_fusion.1), calls=%async_computation.1 | async-start | bytes 8388608 | tf_op jit(solution)/shard_map/all_to_all | solution.py:82
  346.5 10.8 %copy-start.2 = (bf16[1,8,16,64,128]{4,3,2,1,0:T(8,128)(2,1)S(1)}, bf16[1,8,16,64,128]{4,3,2,1,0:T(8,128)(2,1)}, u32[]{:S(2)}) copy-start(bf16[1,8,16,64,128]{4,3,2,1,0:T(8,128)(2,1)} %copy.89) | copy-start | bytes 6291460
  374.9 3.2 copy-start.1
  543.4 5.7 slice-start
  544.6 4.5 slice-start.1
  619.1 82.0 %all-to-all-start.3 = ((bf16[2,128,64,128]{3,2,0,1:T(8,128)(2,1)}), bf16[2,128,64,128]{3,2,0,1:T(8,128)(2,1)}, u32[]{:S(2)}, u32[]{:S(2)}) async-start(bf16[2,128,64,128]{3,2,0,1:T(8,128)(2,1)} %pad_maximum_fusion.3), calls=%async_computation.3 | async-start | bytes 8388608 | tf_op jit(solution)/shard_map/all_to_all | solution.py:82
  736.7 10.7 %copy-start.3 = (bf16[1,8,16,64,128]{4,3,2,1,0:T(8,128)(2,1)S(1)}, bf16[1,8,16,64,128]{4,3,2,1,0:T(8,128)(2,1)}, u32[]{:S(2)}) copy-start(bf16[1,8,16,64,128]{4,3,2,1,0:T(8,128)(2,1)} %copy.111) | copy-start | bytes 6291460
where the time goes:
time: 836 us; the launch traced here: 832 us
  blocking collectives  328 us (39%)
  matrix products  244 us (29%)
  waiting for transfers between devices  138 us (17%)
  local copies, waits for them, and re-layouts  60.7 us (7%)
  other arithmetic  47.7 us (6%)
  starting transfers between devices  9.31 us (1%)
    all_to_all x2, blocking collectives, apply_adjoint(): lax.all_to_all(image, 'freq', split_axis=2, concat_axis=1, tiled=True)  211 us
    all_to_all x2, waiting for transfers between devices, body(): lax.all_to_all(spectrum, 'freq', split_axis=1, concat_axis=2, tiled=True)  138 us
    psum x3, blocking collectives, joint_total(): return lax.psum((first, second, third), 'freq')  117 us
    unnamed x22, local copies, waits for them, and re-layouts  31.8 us
    dot_general x2, matrix products, body(): jnp.einsum('ptx,pxi->pti', kernel_imaginary, solution_real, preferred_ele...  28.3 us
    dot_general x2, matrix products, body(): jnp.einsum('ptx,pxi->pti', kernel_imaginary, solution_imaginary, preferre...  28 us
    dot_general x2, matrix products, invert(): jnp.dot(sin_tab.T, widened[1].reshape(NF, -1), precision=highest)  23.4 us
    dot_general x2, matrix products, body(): jnp.einsum('ptx,pxi->pti', kernel_real, solution_imaginary, preferred_ele...  22.4 us
  transfers between devices with their start and end apart: 2, of which 2 were waited for; matrix products, arithmetic and copies ran while one was open for 2% of the time, Pallas kernels for 0%

commit v1 on v0

--- a/solution.py
+++ b/solution.py
@@ -79,8 +79,11 @@
             .reshape(2, NF, rec_local, focal_count)
             .astype(jnp.bfloat16)
         )
-        multiply_block_in = lax.all_to_all(
-            spectrum, "freq", split_axis=1, concat_axis=2, tiled=True
+        multiply_block_in = jnp.concatenate(
+            jax.lax.all_to_all(
+                jnp.stack(jnp.split(spectrum, jax.lax.psum(1, "freq"), axis=1)), "freq", 0, 0
+            ),
+            axis=2,
         )
         solution_real = multiply_block_in[0]
         solution_imaginary = multiply_block_in[1]

time: 836 us -> 850 us (1.017)
  local copies, waits for them, and re-layouts: 60.7 us -> 80.6 us
    unnamed x22 -> x51, local copies, waits for them, and re-layouts: 31.8 us -> 54.8 us
where the time goes in v1:
time: 850 us; the launch traced here: 846 us
  blocking collectives  328 us (39%)
  matrix products  243 us (29%)
  waiting for transfers between devices  138 us (16%)
  local copies, waits for them, and re-layouts  80.6 us (9%)
  other arithmetic  43.1 us (5%)
  starting transfers between devices  9.31 us (1%)
    all_to_all x2, blocking collectives, apply_adjoint(): lax.all_to_all(image, 'freq', split_axis=2, concat_axis=1, tiled=True)  211 us
    all_to_all x2, waiting for transfers between devices, body(): jax.lax.all_to_all(jnp.stack(jnp.split(spectrum, jax.lax.psum(1, 'freq'),...  138 us
    psum x3, blocking collectives, joint_total(): return lax.psum((first, second, third), 'freq')  117 us
    unnamed x51, local copies, waits for them, and re-layouts  54.8 us
    dot_general x2, matrix products, body(): jnp.einsum('ptx,pxi->pti', kernel_imaginary, solution_real, preferred_ele...  28.1 us
    dot_general x2, matrix products, body(): jnp.einsum('ptx,pxi->pti', kernel_imaginary, solution_imaginary, preferre...  26.9 us
    dot_general x2, matrix products, invert(): jnp.dot(sin_tab.T, widened[1].reshape(NF, -1), precision=highest)  23.4 us
    dot_general x2, matrix products, body(): jnp.einsum('ptx,pxi->pti', kernel_real, solution_imaginary, preferred_ele...  22.4 us
  transfers between devices with their start and end apart: 2, of which 2 were waited for; matrix products, arithmetic and copies ran while one was open for 2% of the time, Pallas kernels for 0%

profile of v1, /device:TPU:0, one launch (start us, length us, event | category | flops | bytes accessed | tf_op | source)
XLA Modules:
  0.0 846.3 jit_solution(6757761371329259270)
XLA Ops:
  8.5 10.8 %fusion.14 = f32[8,1024,128]{2,1,0:T(8,128)} fusion(bf16[2,8,1024,1024]{3,2,1,0:T(8,128)(2,1)} %param.3, bf16[2,8,1024,128]{3,2,1,0:T(8,128)(2,1)S(1)} %get-tuple-element.15), kind=kOutput, calls=%fused_computation.14 | convolution fusion | flops 2147483648 | bytes 23068672 | tf_op jit(solution)/shard_map/hvi,hvg->hig/dot_general | solution.py:51
  19.4 10.7 %fusion.12 = f32[8,1024,128]{2,1,0:T(8,128)} fusion(bf16[2,8,1024,1024]{3,2,1,0:T(8,128)(2,1)} %param.3, bf16[2,8,1024,128]{3,2,1,0:T(8,128)(2,1)S(1)} %get-tuple-element.15), kind=kOutput, calls=%fused_computation.12 | convolution fusion | flops 2147483648 | bytes 23068672 | tf_op jit(solution)/shard_map/hvi,hvg->hig/dot_general | solution.py:56
  39.7 10.4 %fusion.68 = bf16[1,8,1024,128]{3,2,1,0:T(8,128)(2,1)S(1)} fusion(f32[8,1024,128]{2,1,0:T(8,128)} %fusion.12, bf16[2,8,1024,128]{3,2,1,0:T(8,128)(2,1)S(1)} %get-tuple-element.15, bf16[2,8,1024,1024]{3,2,1,0:T(8,128)(2,1)} %param.3), kind=kOutput, calls=%fused_computation.98 | convolution fusion | flops 2149580800 | bytes 25165824 | tf_op jit(solution)/shard_map/hvi,hvg->hig/dot_general | solution.py:54
  53.2 99.3 %all_to_all.40 = bf16[2,8,1024,128]{3,1,0,2:T(8,128)(2,1)S(1)} all-to-all(bf16[2,8,1024,128]{3,1,0,2:T(8,128)(2,1)S(1)} %copy.82), channel_id=1, replica_groups=mesh['grp'=2,'freq'=16] {'freq'}, dimensions={2} | all-to-all | bytes 8388608 | tf_op jit(solution)/shard_map/all_to_all | solution.py:60
  159.0 12.1 %multiply_reduce_fusion.4 = (f32[]{:T(128)}, f32[256,8192]{1,0:T(8,128)}) fusion(s32[8192]{0:T(1024)S(1)} %bitcast.367, f32[256,8192]{1,0:T(8,128)S(1)} %fusion.78, bf16[16,8,64,128]{3,2,1,0:T(8,128)(2,1)S(1)} %get-tuple-element.22), kind=kOutput, calls=%fused_computation.58 | convolution fusion | flops 3232202752 | bytes 18907140 | tf_op jit(solution)/shard_map/dot_general | solution.py:40
  171.1 34.1 %all-reduce.1 = (f32[]{:T(128)}, f32[]{:T(128)}) all-reduce(f32[]{:T(128)} %get-tuple-element.24, f32[]{:T(128)} %get-tuple-element.14), channel_id=1, replica_groups=mesh['grp'=2,'freq'=16] {'freq'}, use_global_device_ids=true, to_apply=%region_1.2 | all-reduce | flops 2 | bytes 16 | tf_op jit(solution)/shard_map/psum | solution.py:24
  206.5 10.7 %fusion.94 = bf16[16,8,64,128]{3,1,2,0:T(8,128)(2,1)S(1)} fusion(s32[8192]{0:T(1024)S(1)} %bitcast.368, f32[256,8192]{1,0:T(8,128)} %get-tuple-element.25, f32[]{:T(128)S(6)} %mul.210), kind=kOutput, calls=%fused_computation.126 | convolution fusion | flops 3232202752 | bytes 10518532 | tf_op jit(solution)/shard_map/dot_general | solution.py:76
  251.2 68.8 %all-to-all-done.1 = bf16[16,2,8,64,128]{4,3,2,1,0:T(8,128)(2,1)} async-done(((bf16[16,2,8,64,128]{4,3,2,1,0:T(8,128)(2,1)}), bf16[16,2,8,64,128]{4,3,2,1,0:T(8,128)(2,1)}, u32[]{:S(2)}, u32[]{:S(2)}) %all-to-all-start.1) | async-done | bytes 4194336 | tf_op jit(solution)/shard_map/all_to_all | solution.py:83
  325.5 13.4 %fusion.10 = f32[8,128,1024]{2,1,0:T(8,128)} fusion(bf16[8,1024,128]{2,1,0:T(8,128)(2,1)S(1)} %bitcast.359, bf16[2,8,1024,1024]{3,2,1,0:T(8,128)(2,1)} %param.3), kind=kOutput, calls=%fused_computation.10 | convolution fusion | flops 2147483648 | bytes 23068672 | tf_op jit(solution)/shard_map/ptx,pxi->pti/dot_general | solution.py:92
  338.9 14.0 %fusion.8 = f32[8,128,1024]{2,1,0:T(8,128)} fusion(bf16[8,1024,128]{2,1,0:T(8,128)(2,1)} %bitcast.363, bf16[2,8,1024,1024]{3,2,1,0:T(8,128)(2,1)} %param.3), kind=kOutput, calls=%fused_computation.8 | convolution fusion | flops 2147483648 | bytes 23068672 | tf_op jit(solution)/shard_map/ptx,pxi->pti/dot_general | solution.py:97
  352.9 10.7 %subtract_bitcast_fusion.1 = f32[1,8,1024,128]{2,3,1,0:T(8,128)S(1)} fusion(f32[8,128,1024]{2,1,0:T(8,128)} %fusion.10, bf16[8,1024,128]{2,1,0:T(8,128)(2,1)} %bitcast.364, bf16[2,8,1024,1024]{3,2,1,0:T(8,128)(2,1)} %param.3), kind=kOutput, calls=%fused_computation.74 | convolution fusion | flops 2148532224 | bytes 27262976 | tf_op jit(solution)/shard_map/ptx,pxi->pti/dot_general | solution.py:90
  363.6 11.2 %add_bitcast_fusion.1 = f32[1,8,1024,128]{2,3,1,0:T(8,128)} fusion(f32[8,128,1024]{2,1,0:T(8,128)} %fusion.8, bf16[8,1024,128]{2,1,0:T(8,128)(2,1)S(1)} %bitcast.360, bf16[2,8,1024,1024]{3,2,1,0:T(8,128)(2,1)} %param.3), kind=kOutput, calls=%fused_computation.73 | convolution fusion | flops 2148532224 | bytes 27262976 | tf_op jit(solution)/shard_map/ptx,pxi->pti/dot_general | solution.py:95
  385.1 10.1 %fusion.6 = f32[8,128,1024]{2,1,0:T(8,128)} fusion(bf16[2,8,1024,1024]{3,2,1,0:T(8,128)(2,1)} %param.3, bf16[2,8,1024,128]{2,3,1,0:T(8,128)(2,1)S(1)} %convert_element_type.32), kind=kOutput, calls=%fused_computation.6 | convolution fusion | flops 2147483648 | bytes 23068672 | tf_op jit(solution)/shard_map/hvi,hvg->hig/dot_general | solution.py:51
  395.2 10.1 %fusion.4 = f32[8,128,1024]{2,1,0:T(8,128)} fusion(bf16[2,8,1024,1024]{3,2,1,0:T(8,128)(2,1)} %param.3, bf16[2,8,1024,128]{2,3,1,0:T(8,128)(2,1)S(1)} %convert_element_type.32), kind=kOutput, calls=%fused_computation.4 | convolution fusion | flops 2147483648 | bytes 23068672 | tf_op jit(solution)/shard_map/hvi,hvg->hig/dot_general | solution.py:56
  414.8 10.8 %fusion.70 = bf16[1,8,1024,128]{2,3,1,0:T(8,128)(2,1)} fusion(f32[8,128,1024]{2,1,0:T(8,128)} %fusion.4, bf16[2,8,1024,1024]{3,2,1,0:T(8,128)(2,1)} %param.3, bf16[2,8,1024,128]{2,3,1,0:T(8,128)(2,1)S(1)} %convert_element_type.32), kind=kOutput, calls=%fused_computation.100 | convolution fusion | flops 2149580800 | bytes 25165824 | tf_op jit(solution)/shard_map/hvi,hvg->hig/dot_general | solution.py:54
  436.5 112.1 %all_to_all.41 = bf16[2,8,1024,128]{3,1,0,2:T(8,128)(2,1)S(1)} all-to-all(bf16[2,8,1024,128]{3,1,0,2:T(8,128)(2,1)} %copy.98), channel_id=1, replica_groups=mesh['grp'=2,'freq'=16] {'freq'}, dimensions={2} | all-to-all | bytes 8388608 | tf_op jit(solution)/shard_map/all_to_all | solution.py:60
  556.0 11.4 %multiply_reduce_fusion = (f32[]{:T(128)}, f32[]{:T(128)}, f32[256,8192]{1,0:T(8,128)}) fusion(s32[8192]{0:T(1024)S(1)} %bitcast.370, f32[]{:T(128)S(6)} %mul.210, f32[256,8192]{1,0:T(8,128)S(1)} %bitcast.348, f32[256,8192]{1,0:T(8,128)S(1)} %fusion.73, bf16[16,8,64,128]{3,2,1,0:T(8,128)(2,1)S(1)} %get-tuple-element.27), kind=kOutput, calls=%fused_computation.53 | convolution fusion | flops 3240591360 | bytes 27295756 | tf_op jit(solution)/shard_map/dot_general | solution.py:40
  567.3 34.2 %all-reduce = (f32[]{:T(128)}, f32[]{:T(128)}, f32[]{:T(128)}) all-reduce(f32[]{:T(128)} %get-tuple-element.12, f32[]{:T(128)} %get-tuple-element.6, f32[]{:T(128)} %get-tuple-element.5), channel_id=1, replica_groups=mesh['grp'=2,'freq'=16] {'freq'}, use_global_device_ids=true, to_apply=%region_5.6 | all-reduce | flops 3 | bytes 24 | tf_op jit(solution)/shard_map/psum | solution.py:24
  648.6 69.0 %all-to-all-done.3 = bf16[16,2,8,64,128]{4,3,2,1,0:T(8,128)(2,1)} async-done(((bf16[16,2,8,64,128]{4,3,2,1,0:T(8,128)(2,1)}), bf16[16,2,8,64,128]{4,3,2,1,0:T(8,128)(2,1)}, u32[]{:S(2)}, u32[]{:S(2)}) %all-to-all-start.3) | async-done | bytes 4194336 | tf_op jit(solution)/shard_map/all_to_all | solution.py:83
  723.1 13.4 %fusion.2 = f32[8,128,1024]{2,1,0:T(8,128)} fusion(bf16[8,1024,128]{2,1,0:T(8,128)(2,1)S(1)} %bitcast.361, bf16[2,8,1024,1024]{3,2,1,0:T(8,128)(2,1)} %param.3), kind=kOutput, calls=%fused_computation.2 | convolution fusion | flops 2147483648 | bytes 23068672 | tf_op jit(solution)/shard_map/ptx,pxi->pti/dot_general | solution.py:92
  736.5 14.1 %fusion = f32[8,128,1024]{2,1,0:T(8,128)} fusion(bf16[8,1024,128]{2,1,0:T(8,128)(2,1)} %bitcast.365, bf16[2,8,1024,1024]{3,2,1,0:T(8,128)(2,1)} %param.3), kind=kOutput, calls=%fused_computation | convolution fusion | flops 2147483648 | bytes 23068672 | tf_op jit(solution)/shard_map/ptx,pxi->pti/dot_general | solution.py:97
  750.6 10.8 %subtract_bitcast_fusion = f32[1,8,1024,128]{2,3,1,0:T(8,128)S(1)} fusion(f32[8,128,1024]{2,1,0:T(8,128)} %fusion.2, bf16[8,1024,128]{2,1,0:T(8,128)(2,1)} %bitcast.366, bf16[2,8,1024,1024]{3,2,1,0:T(8,128)(2,1)} %param.3), kind=kOutput, calls=%fused_computation.70 | convolution fusion | flops 2148532224 | bytes 27262976 | tf_op jit(solution)/shard_map/ptx,pxi->pti/dot_general | solution.py:90
  761.4 11.2 %add_bitcast_fusion = f32[1,8,1024,128]{2,3,1,0:T(8,128)} fusion(f32[8,128,1024]{2,1,0:T(8,128)} %fusion, bf16[8,1024,128]{2,1,0:T(8,128)(2,1)S(1)} %bitcast.362, bf16[2,8,1024,1024]{3,2,1,0:T(8,128)(2,1)} %param.3), kind=kOutput, calls=%fused_computation.69 | convolution fusion | flops 2148532224 | bytes 27262976 | tf_op jit(solution)/shard_map/ptx,pxi->pti/dot_general | solution.py:95
  787.1 48.3 %psum.47 = f32[]{:T(128)} all-reduce(f32[]{:T(128)} %fusion.40), channel_id=1, replica_groups=mesh['grp'=2,'freq'=16] {'freq'}, use_global_device_ids=true, to_apply=%region_11.12 | all-reduce | flops 1 | bytes 8 | tf_op jit(solution)/shard_map/psum | solution.py:24
  (82 shorter events, 179.6 us)
Async XLA Ops:
  154.5 4.4 copy-start.2
  206.5 10.7 %copy-start = (f32[256,8192]{1,0:T(8,128)S(1)}, f32[256,8192]{1,0:T(8,128)}, u32[]{:S(2)}) copy-start(f32[256,8192]{1,0:T(8,128)} %get-tuple-element.25) | copy-start | bytes 25165828
  238.0 82.0 %all-to-all-start.1 = ((bf16[16,2,8,64,128]{4,3,2,1,0:T(8,128)(2,1)}), bf16[16,2,8,64,128]{4,3,2,1,0:T(8,128)(2,1)}, u32[]{:S(2)}, u32[]{:S(2)}) async-start(bf16[16,2,8,64,128]{4,3,2,1,0:T(8,128)(2,1)} %fusion.121), calls=%async_computation.1 | async-start | bytes 8388608 | tf_op jit(solution)/shard_map/all_to_all | solution.py:83
  381.2 3.2 copy-start.1
  550.6 5.3 slice-start
  551.7 4.3 slice-start.1
  635.4 82.2 %all-to-all-start.3 = ((bf16[16,2,8,64,128]{4,3,2,1,0:T(8,128)(2,1)}), bf16[16,2,8,64,128]{4,3,2,1,0:T(8,128)(2,1)}, u32[]{:S(2)}, u32[]{:S(2)}) async-start(bf16[16,2,8,64,128]{4,3,2,1,0:T(8,128)(2,1)} %fusion.105), calls=%async_computation.3 | async-start | bytes 8388608 | tf_op jit(solution)/shard_map/all_to_all | solution.py:83
